TPU v7x, 32 devices: a whole 2x2x4 slice. The times are simulated.
32 devices in a mesh: dp: 4 (over x, core), mp: 8 (over z, y).
Axes of the slice: x: 2, y: 2, z: 4, core: 2. Of those that a mesh axis runs over, the one named last changes fastest.
Arguments:
- tokens: bfloat16 [1024, 8192], P('dp'), may hold values from -6 to 6
- norm_gain: float32 [8192], replicated, may hold values from 0.5 to 1.5
- gate_weight: bfloat16 [8192, 28672], P('dp', 'mp'), may hold values from -0.0625 to 0.0625
- gate_mask: int32 [8192, 896], P('dp', 'mp'), may hold values from -2147483648 to 2147483646
- up_weight: bfloat16 [8192, 28672], P('dp', 'mp'), may hold values from -0.0625 to 0.0625
- up_mask: int32 [8192, 896], P('dp', 'mp'), may hold values from -2147483648 to 2147483646
- down_weight: bfloat16 [28672, 8192], P('mp', 'dp'), may hold values from -0.03125 to 0.03125
- down_mask: int32 [28672, 256], P('mp', 'dp'), may hold values from -2147483648 to 2147483647, as said below
Outputs:
- mixed: bfloat16 [1024, 8192], P('mp', 'dp')
- input_norms: float32 [8192], P('dp')
- hidden_norms: float32 [28672], P('mp')
Inputs may be any that keep to these rules, and one draw needn't show every extreme that they name: `down_mask`: in every word each of the eight aligned groups of four bits holds exactly two ones, so exactly two of every four consecutive columns of the down projection are kept.
All inputs are finite; a program needn't handle non-finite values.
Results may differ from a plain program's by a relative error of at most 0.025.
Values may be sent and summed in bfloat16 or wider, within the bound.
A program may use at most 192 MiB of HBM per device.

v0:
```python
import jax
import jax.numpy as jnp
from jax import lax
from jax.sharding import PartitionSpec as P


def keep_entries(weight, packed):
    shifts = jnp.arange(32, dtype=jnp.int32)
    kept_bits = jnp.right_shift(packed[..., None], shifts) & 1
    kept_bits = kept_bits.reshape(weight.shape)
    return jnp.where(kept_bits == 1, weight, jnp.zeros_like(weight))


def on_device(
    tokens, norm_gain, gate_weight, gate_mask, up_weight, up_mask, down_weight, down_mask
):
    values = tokens.astype(jnp.float32)
    scale = lax.rsqrt(jnp.mean(values * values, axis=1, keepdims=True) + 1e-05)
    normed = (values * scale * norm_gain).astype(jnp.bfloat16)
    columns = lax.all_to_all(normed, "dp", split_axis=1, concat_axis=0, tiled=True)
    widened = columns.astype(jnp.float32)
    input_norms = jnp.sqrt(jnp.sum(widened * widened, axis=0))
    gate_kept = keep_entries(gate_weight, gate_mask)
    up_kept = keep_entries(up_weight, up_mask)
    down_kept = keep_entries(down_weight, down_mask)
    units = gate_kept.shape[1]
    gate_part = jnp.dot(columns, gate_kept, preferred_element_type=jnp.float32)
    up_part = jnp.dot(columns, up_kept, preferred_element_type=jnp.float32)
    both_sums = lax.psum_scatter(
        jnp.concatenate([gate_part, up_part], axis=1).astype(jnp.bfloat16),
        "dp",
        scatter_dimension=0,
        tiled=True,
    ).astype(jnp.float32)
    hidden = (jax.nn.silu(both_sums[:, :units]) * both_sums[:, units:]).astype(jnp.bfloat16)
    wide_hidden = hidden.astype(jnp.float32)
    squares = lax.psum(jnp.sum(wide_hidden * wide_hidden, axis=0), "dp")
    hidden_norms = jnp.sqrt(squares)
    partial_out = jnp.dot(
        lax.all_gather(hidden, "dp", axis=0, tiled=True),
        down_kept,
        preferred_element_type=jnp.float32,
    )
    mixed = lax.psum_scatter(
        partial_out.astype(jnp.bfloat16), "mp", scatter_dimension=0, tiled=True
    )
    return (mixed, input_norms, hidden_norms)


def solution(mesh):
    return jax.shard_map(
        on_device,
        mesh=mesh,
        in_specs=(
            P("dp", None),
            P(),
            P("dp", "mp"),
            P("dp", "mp"),
            P("dp", "mp"),
            P("dp", "mp"),
            P("mp", "dp"),
            P("mp", "dp"),
        ),
        out_specs=(P("mp", "dp"), P("dp"), P("mp")),
        check_vma=False,
    )
```

profile of v0, /device:TPU:0, one launch (start us, length us, event | category | flops | bytes accessed | tf_op | source)
XLA Modules:
  0.0 449.8 jit_solution(9891590436069383037)
XLA Ops:
  7.2 6.4 %copy.17 = bf16[256,8192]{0,1:T(8,128)(2,1)} copy(bf16[256,8192]{1,0:T(8,128)(2,1)} %param.8) | data formatting | bytes 8388608 | tf_op args[0]
  13.6 3.3 fusion.9
  16.9 4.2 fusion.11
  21.0 4.9 %all-to-all-start = ((bf16[256,4,2048]{0,2,1:T(8,128)(2,1)}), bf16[256,4,2048]{0,2,1:T(8,128)(2,1)}, u32[]{:S(2)}, u32[]{:S(2)}) async-start(bf16[256,4,2048]{0,2,1:T(8,128)(2,1)} %bitcast.34), calls=%async_computation | async-start | bytes 8388608 | tf_op jit(solution)/shard_map/all_to_all | solution.py:20
  26.0 0.1 shift_right_arithmetic.63
  26.1 20.3 %copy.19 = bf16[2048,3584]{0,1:T(8,128)(2,1)} copy(bf16[2048,3584]{1,0:T(8,128)(2,1)} %param.10) | data formatting | bytes 29360128 | tf_op args[2]
  46.4 20.5 %copy.20 = bf16[2048,3584]{0,1:T(8,128)(2,1)} copy(bf16[2048,3584]{1,0:T(8,128)(2,1)} %param.12) | data formatting | bytes 29360128 | tf_op args[4]
  66.9 28.4 %fusion.6 = (bf16[2048,3584]{0,1:T(8,128)(2,1)}, bf16[2048,3584]{0,1:T(8,128)(2,1)}) fusion(bf16[2048,3584]{0,1:T(8,128)(2,1)} %copy.19, s32[3584]{0:T(1024)S(1)} %shift_right_arithmetic.63, s32[2048,112]{0,1:T(8,128)S(1)} %copy-done.1, bf16[2048,3584]{0,1:T(8,128)(2,1)} %copy.20, s32[2048,112]{0,1:T(8,128)S(1)} %copy-done.2), kind=kLoop, calls=%fused_computation.9 | loop fusion | flops 58720256 | bytes 60569600 | tf_op jit(solution)/shard_map/jit(_where)/select_n | solution.py:11
  95.3 6.3 %copy.18 = bf16[4,256,2048]{2,1,0:T(8,128)(2,1)} copy(bf16[4,256,2048]{1,2,0:T(8,128)(2,1)} %bitcast.1) | data formatting | bytes 8388608 | tf_op jit(solution)/shard_map/all_to_all | solution.py:20
  101.6 23.7 %convolution_convert_fusion.1 = bf16[1024,3584]{1,0:T(8,128)(2,1)} fusion(bf16[1024,2048]{1,0:T(8,128)(2,1)} %bitcast.35, bf16[2048,3584]{0,1:T(8,128)(2,1)} %get-tuple-element.5), kind=kOutput, calls=%fused_computation.20 | convolution fusion | flops 15036055552 | bytes 26214400 | tf_op jit(solution)/shard_map/dot_general | solution.py:27
  125.3 20.5 %convolution_convert_fusion = bf16[1024,3584]{1,0:T(8,128)(2,1)} fusion(bf16[1024,2048]{1,0:T(8,128)(2,1)S(1)} %bitcast.36, bf16[2048,3584]{0,1:T(8,128)(2,1)} %get-tuple-element.6), kind=kOutput, calls=%fused_computation.19 | convolution fusion | flops 15036055552 | bytes 26214400 | tf_op jit(solution)/shard_map/dot_general | solution.py:28
  145.8 12.6 %pad_maximum_fusion = bf16[1024,7168]{1,0:T(8,128)(2,1)} fusion(bf16[1024,3584]{1,0:T(8,128)(2,1)} %convolution_convert_fusion, bf16[1024,3584]{1,0:T(8,128)(2,1)} %convolution_convert_fusion.1), kind=kLoop, calls=%fused_computation.12 | loop fusion | flops 29360128 | bytes 29360128 | tf_op jit(solution)/shard_map/concatenate | solution.py:30
  158.5 117.2 %reduce-scatter.3.cloned.1.call-done = bf16[256,7168]{1,0:T(8,128)(2,1)} async-done(((bf16[1024,7168]{1,0:T(8,128)(2,1)}), bf16[256,7168]{1,0:T(8,128)(2,1)}) %reduce-scatter.3.cloned.1.call-update) | async-done | bytes 3670032 | tf_op jit(solution)/shard_map/reduce_scatter | solution.py:29
  275.7 2.9 convert_element_type.25
  278.6 2.5 multiply_reduce_fusion.1
  281.3 19.5 %copy.21 = bf16[3584,2048]{0,1:T(8,128)(2,1)} copy(bf16[3584,2048]{1,0:T(8,128)(2,1)} %param.14) | data formatting | bytes 29360128 | tf_op args[6]
  300.8 15.1 %fusion.8 = bf16[3584,2048]{0,1:T(8,128)(2,1)} fusion(bf16[3584,2048]{0,1:T(8,128)(2,1)} %copy.21, s32[2048]{0:T(1024)S(1)} %shift_right_arithmetic.72, s32[3584,64]{0,1:T(8,128)S(1)} %copy-done.3), kind=kLoop, calls=%fused_computation.11 | loop fusion | flops 29360128 | bytes 30285824 | tf_op jit(solution)/shard_map/jit(_where)/select_n | solution.py:11
  315.9 17.7 %all-gather.2.cloned.1.call-done = bf16[1024,3584]{1,0:T(8,128)(2,1)} async-done(((bf16[256,3584]{1,0:T(8,128)(2,1)}), bf16[1024,3584]{1,0:T(8,128)(2,1)}) %all-gather.2.cloned.1.call-update) | async-done | bytes 7340048 | tf_op jit(solution)/shard_map/all_gather | solution.py:40
  333.6 21.2 %convolution_convert_fusion.2 = bf16[1024,2048]{1,0:T(8,128)(2,1)} fusion(bf16[1024,3584]{1,0:T(8,128)(2,1)} %all-gather.2.cloned.1.call-done, bf16[3584,2048]{0,1:T(8,128)(2,1)} %fusion.8), kind=kOutput, calls=%fused_computation.21 | convolution fusion | flops 15034482688 | bytes 26214400 | tf_op jit(solution)/shard_map/dot_general | solution.py:39
  354.9 3.1 multiply_reduce_fusion
  357.9 0.6 sqrt.6
  358.6 10.6 %psum.7 = f32[3584]{0:T(1024)S(1)} all-reduce(f32[3584]{0:T(1024)S(1)} %get-tuple-element.3), channel_id=1, replica_groups=mesh['dp'=4,'mp'=8] {'dp'}, use_global_device_ids=true, to_apply=%region_5.6 | all-reduce | flops 3584 | bytes 28672 | tf_op jit(solution)/shard_map/psum | solution.py:37
  369.2 0.6 sqrt.7
  369.8 73.5 %reduce-scatter.5.cloned.1.call-done = bf16[128,2048]{1,0:T(8,128)(2,1)} async-done(((bf16[1024,2048]{1,0:T(8,128)(2,1)}), bf16[128,2048]{1,0:T(8,128)(2,1)}) %reduce-scatter.5.cloned.1.call-update) | async-done | bytes 524304 | tf_op jit(solution)/shard_map/reduce_scatter | solution.py:44
  (21 shorter events, 0.3 us)
Async XLA Ops:
  7.2 9.7 %copy-start.4 = (f32[8192]{0:T(1024)S(1)}, f32[8192]{0:T(1024)}, u32[]{:S(2)}) copy-start(f32[8192]{0:T(1024)} %param.9) | copy-start | bytes 98308
  21.0 74.2 %all-to-all-start = ((bf16[256,4,2048]{0,2,1:T(8,128)(2,1)}), bf16[256,4,2048]{0,2,1:T(8,128)(2,1)}, u32[]{:S(2)}, u32[]{:S(2)}) async-start(bf16[256,4,2048]{0,2,1:T(8,128)(2,1)} %bitcast.34), calls=%async_computation | async-start | bytes 8388608 | tf_op jit(solution)/shard_map/all_to_all | solution.py:20
  25.9 249.8 %reduce-scatter.3.cloned.1.call-start = ((), (), s32[]{:S(2)}) async-start(), calls=%async_computation.3 | async-start | bytes 18350080 | tf_op jit(solution)/shard_map/reduce_scatter | solution.py:29
  46.4 20.5 %copy-start.1 = (s32[2048,112]{0,1:T(8,128)S(1)}, s32[2048,112]{0,1:T(8,128)}, u32[]{:S(2)}) copy-start(s32[2048,112]{0,1:T(8,128)} %param.11) | copy-start | bytes 2752516
  46.4 20.5 %copy-start.2 = (s32[2048,112]{0,1:T(8,128)S(1)}, s32[2048,112]{0,1:T(8,128)}, u32[]{:S(2)}) copy-start(s32[2048,112]{0,1:T(8,128)} %param.13) | copy-start | bytes 2752516
  101.6 23.7 %copy-start = (bf16[4,256,2048]{2,1,0:T(8,128)(2,1)S(1)}, bf16[4,256,2048]{2,1,0:T(8,128)(2,1)}, u32[]{:S(2)}) copy-start(bf16[4,256,2048]{2,1,0:T(8,128)(2,1)} %copy.18) | copy-start | bytes 12582916
  158.5 175.2 %all-gather.2.cloned.1.call-start = ((), (), s32[]{:S(2)}) async-start(), calls=%async_computation.4 | async-start | bytes 9175040 | tf_op jit(solution)/shard_map/all_gather | solution.py:40
  281.2 162.1 %reduce-scatter.5.cloned.1.call-start = ((), (), s32[]{:S(2)}) async-start(), calls=%async_computation.5 | async-start | bytes 4718592 | tf_op jit(solution)/shard_map/reduce_scatter | solution.py:44
  281.3 19.5 %copy-start.3 = (s32[3584,64]{0,1:T(8,128)S(1)}, s32[3584,64]{0,1:T(8,128)}, u32[]{:S(2)}) copy-start(s32[3584,64]{0,1:T(8,128)} %param.15) | copy-start | bytes 2752516
Sparse Core Ops, SparseCore 0:
  158.6 117.0 reduce-scatter.2
  281.3 52.2 all-gather.1
  355.0 88.2 reduce-scatter.4
where the time goes:
time: 452 us; the launch traced here: 450 us
  waiting for transfers between devices  208 us (46%)
  local copies, waits for them, and re-layouts  74.5 us (16%)
  other arithmetic  72 us (16%)
  matrix products  65.4 us (14%)
  between operations  13.8 us (3%)
  blocking collectives  10.6 us (2%)
  starting transfers between devices  5.01 us (1%)
    reduce_scatter x1, waiting for transfers between devices, on_device(): lax.psum_scatter(jnp.concatenate([gate_part, up_part], axis=1).astype(jnp...  117 us
    reduce_scatter x1, waiting for transfers between devices, on_device(): lax.psum_scatter(partial_out.astype(jnp.bfloat16), 'mp', scatter_dimensio...  73.5 us
    unnamed x14, local copies, waits for them, and re-layouts  66.7 us
    select_n x2, other arithmetic, keep_entries(): return jnp.where(kept_bits == 1, weight, jnp.zeros_like(weight))  43.5 us
    dot_general x1, matrix products, on_device(): gate_part = jnp.dot(columns, gate_kept, preferred_element_type=jnp.float32)  23.7 us
    dot_general x1, matrix products, on_device(): jnp.dot(lax.all_gather(hidden, 'dp', axis=0, tiled=True), down_kept, pref...  21.2 us
    dot_general x1, matrix products, on_device(): up_part = jnp.dot(columns, up_kept, preferred_element_type=jnp.float32)  20.5 us
    all_gather x1, waiting for transfers between devices, on_device(): lax.all_gather(hidden, 'dp', axis=0, tiled=True)  17.7 us
  transfers between devices with their start and end apart: 4, of which 3 were waited for; matrix products, arithmetic and copies ran while one was open for 24% of the time, Pallas kernels for 0%

commit v1 on v0

--- a/solution.py
+++ b/solution.py
@@ -37,7 +37,9 @@
     squares = lax.psum(jnp.sum(wide_hidden * wide_hidden, axis=0), "dp")
     hidden_norms = jnp.sqrt(squares)
     partial_out = jnp.dot(
-        lax.all_gather(hidden, "dp", axis=0, tiled=True),
+        jnp.concatenate(
+            lax.all_to_all(jnp.stack([hidden] * lax.axis_size("dp")), "dp", 0, 0), axis=0
+        ),
         down_kept,
         preferred_element_type=jnp.float32,
     )

time: 452 us -> 490 us (1.084)
  waiting for transfers between devices: 208 us -> 239 us
  starting transfers between devices: 5.01 us -> 10.4 us
    all_to_all x0 -> x1, waiting for transfers between devices: none -> 47.7 us  [on_device(): lax.all_to_all(jnp.stack([hidden] * lax.axis_size('dp')), 'dp', 0, 0)]
    all_gather x1 -> x0, waiting for transfers between devices: 17.7 us -> none  [on_device(): lax.all_gather(hidden, 'dp', axis=0, tiled=True)]
    all_to_all x0 -> x1, starting transfers between devices: none -> 5.43 us  [on_device(): lax.all_to_all(jnp.stack([hidden] * lax.axis_size('dp')), 'dp', 0, 0)]
  transfers between devices with their start and end apart: 4 -> 4, of which waited for: 3 -> 3; matrix products, arithmetic and copies ran while one was open for 24% -> 22% of each run, Pallas kernels for 0% -> 0%
where the time goes in v1:
time: 490 us; the launch traced here: 487 us
  waiting for transfers between devices  239 us (49%)
  local copies, waits for them, and re-layouts  77.4 us (16%)
  other arithmetic  70.8 us (14%)
  matrix products  65.5 us (13%)
  between operations  14.1 us (3%)
  blocking collectives  10.5 us (2%)
  starting transfers between devices  10.4 us (2%)
    reduce_scatter x1, waiting for transfers between devices, on_device(): lax.psum_scatter(jnp.concatenate([gate_part, up_part], axis=1).astype(jnp...  117 us
    reduce_scatter x1, waiting for transfers between devices, on_device(): lax.psum_scatter(partial_out.astype(jnp.bfloat16), 'mp', scatter_dimensio...  73.6 us
    unnamed x14, local copies, waits for them, and re-layouts  66.2 us
    all_to_all x1, waiting for transfers between devices, on_device(): lax.all_to_all(jnp.stack([hidden] * lax.axis_size('dp')), 'dp', 0, 0)  47.7 us
    select_n x2, other arithmetic, keep_entries(): return jnp.where(kept_bits == 1, weight, jnp.zeros_like(weight))  43.4 us
    dot_general x1, matrix products, on_device(): gate_part = jnp.dot(columns, gate_kept, preferred_element_type=jnp.float32)  23.7 us
    dot_general x1, matrix products, on_device(): jnp.dot(jnp.concatenate(lax.all_to_all(jnp.stack([hidden] * lax.axis_size...  21.2 us
    dot_general x1, matrix products, on_device(): up_part = jnp.dot(columns, up_kept, preferred_element_type=jnp.float32)  20.6 us
  transfers between devices with their start and end apart: 4, of which 3 were waited for; matrix products, arithmetic and copies ran while one was open for 22% of the time, Pallas kernels for 0%

profile of v1, /device:TPU:0, one launch (start us, length us, event | category | flops | bytes accessed | tf_op | source)
XLA Modules:
  0.0 487.3 jit_solution(17206727851068658818)
XLA Ops:
  7.2 6.4 %copy.17 = bf16[256,8192]{0,1:T(8,128)(2,1)} copy(bf16[256,8192]{1,0:T(8,128)(2,1)} %param.8) | data formatting | bytes 8388608 | tf_op args[0]
  13.6 3.3 fusion.9
  16.9 4.2 fusion.11
  21.0 4.9 %all-to-all-start = ((bf16[256,4,2048]{0,2,1:T(8,128)(2,1)}), bf16[256,4,2048]{0,2,1:T(8,128)(2,1)}, u32[]{:S(2)}, u32[]{:S(2)}) async-start(bf16[256,4,2048]{0,2,1:T(8,128)(2,1)} %bitcast.35), calls=%async_computation | async-start | bytes 8388608 | tf_op jit(solution)/shard_map/all_to_all | solution.py:20
  26.1 20.2 %copy.19 = bf16[2048,3584]{0,1:T(8,128)(2,1)} copy(bf16[2048,3584]{1,0:T(8,128)(2,1)} %param.10) | data formatting | bytes 29360128 | tf_op args[2]
  46.3 20.5 %copy.20 = bf16[2048,3584]{0,1:T(8,128)(2,1)} copy(bf16[2048,3584]{1,0:T(8,128)(2,1)} %param.12) | data formatting | bytes 29360128 | tf_op args[4]
  66.8 28.4 %fusion.6 = (bf16[2048,3584]{0,1:T(8,128)(2,1)}, bf16[2048,3584]{0,1:T(8,128)(2,1)}) fusion(bf16[2048,3584]{0,1:T(8,128)(2,1)} %copy.19, s32[3584]{0:T(1024)S(1)} %shift_right_arithmetic.63, s32[2048,112]{0,1:T(8,128)S(1)} %copy-done.1, bf16[2048,3584]{0,1:T(8,128)(2,1)} %copy.20, s32[2048,112]{0,1:T(8,128)S(1)} %copy-done.2), kind=kLoop, calls=%fused_computation.9 | loop fusion | flops 58720256 | bytes 60569600 | tf_op jit(solution)/shard_map/jit(_where)/select_n | solution.py:11
  95.2 6.3 %copy.18 = bf16[4,256,2048]{2,1,0:T(8,128)(2,1)} copy(bf16[4,256,2048]{1,2,0:T(8,128)(2,1)} %bitcast.1) | data formatting | bytes 8388608 | tf_op jit(solution)/shard_map/all_to_all | solution.py:20
  101.5 23.7 %convolution_convert_fusion.1 = bf16[1024,3584]{1,0:T(8,128)(2,1)} fusion(bf16[1024,2048]{1,0:T(8,128)(2,1)} %bitcast.36, bf16[2048,3584]{0,1:T(8,128)(2,1)} %get-tuple-element.5), kind=kOutput, calls=%fused_computation.20 | convolution fusion | flops 15036055552 | bytes 26214400 | tf_op jit(solution)/shard_map/dot_general | solution.py:27
  125.2 20.6 %convolution_convert_fusion = bf16[1024,3584]{1,0:T(8,128)(2,1)} fusion(bf16[1024,2048]{1,0:T(8,128)(2,1)S(1)} %bitcast.37, bf16[2048,3584]{0,1:T(8,128)(2,1)} %get-tuple-element.6), kind=kOutput, calls=%fused_computation.19 | convolution fusion | flops 15036055552 | bytes 26214400 | tf_op jit(solution)/shard_map/dot_general | solution.py:28
  145.8 12.6 %pad_maximum_fusion = bf16[1024,7168]{1,0:T(8,128)(2,1)} fusion(bf16[1024,3584]{1,0:T(8,128)(2,1)} %convolution_convert_fusion, bf16[1024,3584]{1,0:T(8,128)(2,1)} %convolution_convert_fusion.1), kind=kLoop, calls=%fused_computation.12 | loop fusion | flops 29360128 | bytes 29360128 | tf_op jit(solution)/shard_map/concatenate | solution.py:30
  158.4 117.3 %reduce-scatter.3.cloned.1.call-done = bf16[256,7168]{1,0:T(8,128)(2,1)} async-done(((bf16[1024,7168]{1,0:T(8,128)(2,1)}), bf16[256,7168]{1,0:T(8,128)(2,1)}) %reduce-scatter.3.cloned.1.call-update) | async-done | bytes 3670032 | tf_op jit(solution)/shard_map/reduce_scatter | solution.py:29
  275.7 2.9 convert_element_type.25
  278.6 1.3 multiply_reduce_fusion.1
  279.9 3.5 stack.2
  283.4 5.4 %all-to-all-start.1 = ((bf16[4,256,3584]{2,1,0:T(8,128)(2,1)}), bf16[4,256,3584]{2,1,0:T(8,128)(2,1)}, u32[]{:S(2)}, u32[]{:S(2)}) async-start(bf16[4,256,3584]{2,1,0:T(8,128)(2,1)} %stack.2), calls=%async_computation.2 | async-start | bytes 14680064 | tf_op jit(solution)/shard_map/all_to_all | solution.py:41
  289.0 19.1 %copy.21 = bf16[3584,2048]{0,1:T(8,128)(2,1)} copy(bf16[3584,2048]{1,0:T(8,128)(2,1)} %param.14) | data formatting | bytes 29360128 | tf_op args[6]
  308.1 15.1 %fusion.8 = bf16[3584,2048]{0,1:T(8,128)(2,1)} fusion(bf16[3584,2048]{0,1:T(8,128)(2,1)} %copy.21, s32[2048]{0:T(1024)S(1)} %shift_right_arithmetic.72, s32[3584,64]{0,1:T(8,128)S(1)} %copy-done.3), kind=kLoop, calls=%fused_computation.11 | loop fusion | flops 29360128 | bytes 30285824 | tf_op jit(solution)/shard_map/jit(_where)/select_n | solution.py:11
  323.1 47.7 %all-to-all-done.1 = bf16[4,256,3584]{2,1,0:T(8,128)(2,1)} async-done(((bf16[4,256,3584]{2,1,0:T(8,128)(2,1)}), bf16[4,256,3584]{2,1,0:T(8,128)(2,1)}, u32[]{:S(2)}, u32[]{:S(2)}) %all-to-all-start.1) | async-done | bytes 7340064 | tf_op jit(solution)/shard_map/all_to_all | solution.py:41
  370.8 21.2 %convolution_convert_fusion.2 = bf16[1024,2048]{1,0:T(8,128)(2,1)} fusion(bf16[1024,3584]{1,0:T(8,128)(2,1)} %bitcast.5, bf16[3584,2048]{0,1:T(8,128)(2,1)} %fusion.8), kind=kOutput, calls=%fused_computation.21 | convolution fusion | flops 15034482688 | bytes 26214400 | tf_op jit(solution)/shard_map/dot_general | solution.py:39
  392.0 3.1 multiply_reduce_fusion
  395.7 10.5 %psum.7 = f32[3584]{0:T(1024)S(1)} all-reduce(f32[3584]{0:T(1024)S(1)} %get-tuple-element.3), channel_id=1, replica_groups=mesh['dp'=4,'mp'=8] {'dp'}, use_global_device_ids=true, to_apply=%region_5.6 | all-reduce | flops 3584 | bytes 28672 | tf_op jit(solution)/shard_map/psum | solution.py:37
  406.2 0.6 sqrt.7
  406.8 73.6 %reduce-scatter.5.cloned.1.call-done = bf16[128,2048]{1,0:T(8,128)(2,1)} async-done(((bf16[1024,2048]{1,0:T(8,128)(2,1)}), bf16[128,2048]{1,0:T(8,128)(2,1)}) %reduce-scatter.5.cloned.1.call-update) | async-done | bytes 524304 | tf_op jit(solution)/shard_map/reduce_scatter | solution.py:46
  (21 shorter events, 0.9 us)
Async XLA Ops:
  7.2 9.7 %copy-start.4 = (f32[8192]{0:T(1024)S(1)}, f32[8192]{0:T(1024)}, u32[]{:S(2)}) copy-start(f32[8192]{0:T(1024)} %param.9) | copy-start | bytes 98308
  21.0 74.2 %all-to-all-start = ((bf16[256,4,2048]{0,2,1:T(8,128)(2,1)}), bf16[256,4,2048]{0,2,1:T(8,128)(2,1)}, u32[]{:S(2)}, u32[]{:S(2)}) async-start(bf16[256,4,2048]{0,2,1:T(8,128)(2,1)} %bitcast.35), calls=%async_computation | async-start | bytes 8388608 | tf_op jit(solution)/shard_map/all_to_all | solution.py:20
  25.9 249.8 %reduce-scatter.3.cloned.1.call-start = ((), (), s32[]{:S(2)}) async-start(), calls=%async_computation.4 | async-start | bytes 18350080 | tf_op jit(solution)/shard_map/reduce_scatter | solution.py:29
  46.3 20.5 %copy-start.1 = (s32[2048,112]{0,1:T(8,128)S(1)}, s32[2048,112]{0,1:T(8,128)}, u32[]{:S(2)}) copy-start(s32[2048,112]{0,1:T(8,128)} %param.11) | copy-start | bytes 2752516
  46.3 20.5 %copy-start.2 = (s32[2048,112]{0,1:T(8,128)S(1)}, s32[2048,112]{0,1:T(8,128)}, u32[]{:S(2)}) copy-start(s32[2048,112]{0,1:T(8,128)} %param.13) | copy-start | bytes 2752516
  101.5 23.7 %copy-start = (bf16[4,256,2048]{2,1,0:T(8,128)(2,1)S(1)}, bf16[4,256,2048]{2,1,0:T(8,128)(2,1)}, u32[]{:S(2)}) copy-start(bf16[4,256,2048]{2,1,0:T(8,128)(2,1)} %copy.18) | copy-start | bytes 12582916
  283.4 87.3 %all-to-all-start.1 = ((bf16[4,256,3584]{2,1,0:T(8,128)(2,1)}), bf16[4,256,3584]{2,1,0:T(8,128)(2,1)}, u32[]{:S(2)}, u32[]{:S(2)}) async-start(bf16[4,256,3584]{2,1,0:T(8,128)(2,1)} %stack.2), calls=%async_computation.2 | async-start | bytes 14680064 | tf_op jit(solution)/shard_map/all_to_all | solution.py:41
  288.9 191.6 %reduce-scatter.5.cloned.1.call-start = ((), (), s32[]{:S(2)}) async-start(), calls=%async_computation.5 | async-start | bytes 4718592 | tf_op jit(solution)/shard_map/reduce_scatter | solution.py:46
  289.0 19.1 %copy-start.3 = (s32[3584,64]{0,1:T(8,128)S(1)}, s32[3584,64]{0,1:T(8,128)}, u32[]{:S(2)}) copy-start(s32[3584,64]{0,1:T(8,128)} %param.15) | copy-start | bytes 2752516
Sparse Core Ops, SparseCore 0:
  158.6 117.0 reduce-scatter.2
  392.1 88.2 reduce-scatter.4
